TPU v7x, 32 devices: a whole 2x2x4 slice. The times are simulated.
32 devices in a mesh: client: 16 (over z, y, core), tp: 2 (over x).
Axes of the slice: x: 2, y: 2, z: 4, core: 2. Of those that a mesh axis runs over, the one named last changes fastest.
Arguments:
- tokens: bfloat16 [4096, 2048], P('client'), may hold values from -6 to 6
- targets: bfloat16 [4096, 2048], P('client'), may hold values from -6 to 6
- norm_gain: float32 [2048], replicated, may hold values from 0.25 to 1.75
- up_frozen: bfloat16 [2048, 7168], P('client', 'tp'), may hold values from -0.125 to 0.125
- down_frozen: bfloat16 [7168, 2048], P('tp', 'client'), may hold values from -0.0625 to 0.0625
- up_left: float32 [16, 2048], replicated, may hold values from -1 to 1
- up_right: float32 [16, 7168], P(None, 'tp'), may hold values from -0.4375 to 0.4375
- down_left: float32 [16, 7168], P(None, 'tp'), may hold values from -0.625 to 0.625
- down_right: float32 [16, 2048], replicated, may hold values from -0.0625 to 0.0625
- counts: int32 [16], P('client'), may hold values from 64 to 4096
Outputs:
- round_up_left: float32 [16, 2048], replicated
- round_up_right: float32 [16, 7168], P(None, 'tp')
- round_down_left: float32 [16, 7168], P(None, 'tp')
- round_down_right: float32 [16, 2048], replicated
All inputs are finite; a program needn't handle non-finite values.
Results may differ from a plain program's by a relative error of at most 0.0089.
Values may be sent and summed in bfloat16 or wider, within the bound.
A program may use at most 128 MiB of HBM per device.

v0:
```python
import jax
import jax.numpy as jnp
from jax import lax
from jax.sharding import PartitionSpec as P

STEPS = 3
LEARN_RATE = 0.01
PROX_WEIGHT = 10.0
ADAPTER_SCALING = 0.5
NORM_EPS = 1e-05


def contracted_rows(left, right):
    return lax.dot_general(
        left, right, (((0,), (0,)), ((), ())), preferred_element_type=jnp.float32
    )


def contract_columns(left, right):
    return lax.dot_general(
        left, right, (((1,), (1,)), ((), ())), preferred_element_type=jnp.float32
    )


def update(value, grad, anchor):
    return value - LEARN_RATE * (grad + PROX_WEIGHT * (value - anchor))


def per_device(
    tokens,
    targets,
    norm_gain,
    up_frozen,
    down_frozen,
    up_left,
    up_right,
    down_left,
    down_right,
    counts,
):
    token_count = tokens.shape[0]
    wide = tokens.astype(jnp.float32)
    scale = lax.rsqrt(jnp.mean(wide * wide, axis=1, keepdims=True) + NORM_EPS)
    normalized_input = (wide * scale * norm_gain).astype(jnp.bfloat16)
    whole_up = lax.all_gather(up_frozen, "client", axis=0, tiled=True)
    frozen_hidden_rows = jnp.dot(normalized_input, whole_up, preferred_element_type=jnp.float32)
    whole_down = lax.all_gather(down_frozen, "client", axis=1, tiled=True)
    start = (up_left, up_right, down_left, down_right)
    params = start
    for local_step in range(STEPS):
        up_left_b = params[0].astype(jnp.bfloat16)
        up_right_batch = params[1].astype(jnp.bfloat16)
        down_left_b = params[2].astype(jnp.bfloat16)
        down_right_batch = params[3].astype(jnp.bfloat16)
        up_low_product = contract_columns(normalized_input, up_left_b).astype(jnp.bfloat16)
        hidden_preactivation = frozen_hidden_rows + ADAPTER_SCALING * jnp.dot(
            up_low_product, up_right_batch, preferred_element_type=jnp.float32
        )
        gated_hidden = jax.nn.silu(hidden_preactivation).astype(jnp.bfloat16)
        partial_value = jnp.dot(gated_hidden, whole_down, preferred_element_type=jnp.float32)
        low_part = contract_columns(gated_hidden, down_left_b)
        share_width = partial_value.shape[1] // lax.axis_size("tp")
        offset = lax.axis_index("tp") * share_width
        summed = lax.psum_scatter(partial_value, "tp", scatter_dimension=1, tiled=True)
        down_low_product = lax.psum(low_part, "tp").astype(jnp.bfloat16)
        right_share = lax.dynamic_slice_in_dim(down_right_batch, offset, share_width, 1)
        token_share = lax.dynamic_slice_in_dim(tokens, offset, share_width, 1)
        target_share = lax.dynamic_slice_in_dim(targets, offset, share_width, 1)
        layer_output = token_share.astype(jnp.float32) + summed
        layer_output = layer_output + ADAPTER_SCALING * jnp.dot(
            down_low_product, right_share, preferred_element_type=jnp.float32
        )
        d_share = ((layer_output - target_share.astype(jnp.float32)) / token_count).astype(
            jnp.bfloat16
        )
        output_gradient = lax.all_gather(d_share, "tp", axis=1, tiled=True)
        down_low_gradient = (
            ADAPTER_SCALING * contract_columns(output_gradient, down_right_batch)
        ).astype(jnp.bfloat16)
        d_gated = contract_columns(output_gradient, whole_down) + jnp.dot(
            down_low_gradient, down_left_b, preferred_element_type=jnp.float32
        )
        sigmoid_pre = jax.nn.sigmoid(hidden_preactivation)
        hidden_gradient = (
            d_gated * sigmoid_pre * (1.0 + hidden_preactivation * (1.0 - sigmoid_pre))
        ).astype(jnp.bfloat16)
        low_rank_gradient = lax.psum(
            ADAPTER_SCALING * contract_columns(hidden_gradient, up_right_batch), "tp"
        )
        up_low_gradient = low_rank_gradient.astype(jnp.bfloat16)
        gradient_tree = (
            contracted_rows(up_low_gradient, normalized_input),
            ADAPTER_SCALING * contracted_rows(up_low_product, hidden_gradient),
            contracted_rows(down_low_gradient, gated_hidden),
            ADAPTER_SCALING * contracted_rows(down_low_product, output_gradient),
        )
        params = jax.tree.map(update, params, gradient_tree, start)
    weight = counts.astype(jnp.float32)

    def weighted(anchor, value):
        return weight[0] * (anchor - value)

    deltas = jax.tree.map(weighted, start, params)
    sums = lax.psum((deltas[0], deltas[1], deltas[2], deltas[3], weight), "client")
    factor = LEARN_RATE * sums[4][0]
    return (sums[0] / factor, sums[1] / factor, sums[2] / factor, sums[3] / factor)


def solution(mesh):
    placed = (
        P("client", None),
        P("client", None),
        P(),
        P("client", "tp"),
        P("tp", "client"),
        P(),
        P(None, "tp"),
        P(None, "tp"),
        P(),
        P("client"),
    )
    return jax.shard_map(
        per_device,
        mesh=mesh,
        in_specs=placed,
        out_specs=(P(), P(None, "tp"), P(None, "tp"), P()),
        check_vma=False,
    )
```

profile of v0, /device:TPU:0, one launch (start us, length us, event | category | flops | bytes accessed | tf_op | source)
XLA Modules:
  0.0 624.4 jit_solution(11934358948694620464)
XLA Ops:
  11.9 114.4 %all-gather.6.cloned.1.call-done = bf16[2048,3584]{1,0:T(8,128)(2,1)} async-done(((bf16[128,3584]{1,0:T(8,128)(2,1)}), bf16[2048,3584]{1,0:T(8,128)(2,1)}) %all-gather.6.cloned.1.call-update) | async-done | bytes 14680080 | tf_op jit(solution)/shard_map/all_gather | solution.py:45
  126.4 7.4 %fusion.104 = f32[256,3584]{1,0:T(8,128)S(1)} fusion(bf16[2048,3584]{1,0:T(8,128)(2,1)} %all-gather.6.cloned.1.call-done, bf16[256,2048]{1,0:T(8,128)(2,1)S(1)} %copy-done.3, f32[2048]{0:T(1024)S(1)} %copy-done.30, f32[256]{0:T(256)S(1)} %add_rsqrt_fusion), kind=kOutput, calls=%fused_computation.147 | convolution fusion | flops 3760193536 | bytes 19407872 | tf_op jit(solution)/shard_map/dot_general | solution.py:46
  138.7 104.7 %all-gather.8.cloned.1.call-done = bf16[3584,2048]{1,0:T(8,128)(2,1)} async-done(((bf16[3584,128]{1,0:T(8,128)(2,1)}), bf16[3584,2048]{1,0:T(8,128)(2,1)}) %all-gather.8.cloned.1.call-update) | async-done | bytes 14680080 | tf_op jit(solution)/shard_map/all_gather | solution.py:47
  243.4 8.8 %fusion.108 = f32[256,2048]{1,0:T(8,128)} fusion(bf16[256,3584]{1,0:T(8,128)(2,1)S(1)} %get-tuple-element.8, bf16[3584,2048]{1,0:T(8,128)(2,1)} %all-gather.8.cloned.1.call-done), kind=kOutput, calls=%fused_computation.150 | convolution fusion | flops 3758096384 | bytes 18612224 | tf_op jit(solution)/shard_map/dot_general | solution.py:60
  253.5 9.4 %psum.77 = bf16[256,16]{0,1:T(8,128)(2,1)S(1)} all-reduce(f32[256,16]{0,1:T(8,128)} %fusion.79), channel_id=1, replica_groups=mesh['client'=16,'tp'=2] {'tp'}, use_global_device_ids=true, to_apply=%region_2.3 | all-reduce | flops 4096 | bytes 24576 | tf_op jit(solution)/shard_map/psum | solution.py:65
  262.9 19.8 %reduce-scatter.4.cloned.1.call-done = f32[256,1024]{1,0:T(8,128)} async-done(((f32[256,2048]{1,0:T(8,128)}), f32[256,1024]{1,0:T(8,128)}) %reduce-scatter.4.cloned.1.call-update) | async-done | bytes 1048592 | tf_op jit(solution)/shard_map/reduce_scatter | solution.py:64
  285.3 21.2 %all-gather.10.cloned.1.call-done = bf16[256,2048]{1,0:T(8,128)(2,1)} async-done(((bf16[256,1024]{1,0:T(8,128)(2,1)}), bf16[256,2048]{1,0:T(8,128)(2,1)}) %all-gather.10.cloned.1.call-update) | async-done | bytes 1048592 | tf_op jit(solution)/shard_map/all_gather | solution.py:76
  306.5 9.5 %fusion.109 = f32[256,3584]{1,0:T(8,128)S(1)} fusion(bf16[256,2048]{1,0:T(8,128)(2,1)} %all-gather.10.cloned.1.call-done, bf16[3584,2048]{1,0:T(8,128)(2,1)} %all-gather.8.cloned.1.call-done), kind=kOutput, calls=%fused_computation.151 | convolution fusion | flops 3758096384 | bytes 19398656 | tf_op jit(solution)/shard_map/dot_general | solution.py:20
  321.7 7.0 %psum.78 = bf16[256,16]{0,1:T(8,128)(2,1)S(1)} all-reduce(f32[256,16]{0,1:T(8,128)S(1)} %convolution_multiply_fusion.16), channel_id=1, replica_groups=mesh['client'=16,'tp'=2] {'tp'}, use_global_device_ids=true, to_apply=%region_3.4 | all-reduce | flops 4096 | bytes 24576 | tf_op jit(solution)/shard_map/psum | solution.py:87
  334.1 8.7 %fusion.110 = f32[256,2048]{1,0:T(8,128)} fusion(bf16[256,3584]{1,0:T(8,128)(2,1)S(1)} %get-tuple-element.10, bf16[3584,2048]{1,0:T(8,128)(2,1)} %all-gather.8.cloned.1.call-done), kind=kOutput, calls=%fused_computation.152 | convolution fusion | flops 3758096384 | bytes 18612224 | tf_op jit(solution)/shard_map/dot_general | solution.py:60
  345.9 8.8 %psum.79 = bf16[256,16]{0,1:T(8,128)(2,1)S(1)} all-reduce(f32[256,16]{0,1:T(8,128)S(1)} %fusion.74), channel_id=1, replica_groups=mesh['client'=16,'tp'=2] {'tp'}, use_global_device_ids=true, to_apply=%region_5.6 | all-reduce | flops 4096 | bytes 24576 | tf_op jit(solution)/shard_map/psum | solution.py:65
  356.9 19.2 %reduce-scatter.6.cloned.1.call-done = f32[256,1024]{1,0:T(8,128)} async-done(((f32[256,2048]{1,0:T(8,128)}), f32[256,1024]{1,0:T(8,128)}) %reduce-scatter.6.cloned.1.call-update) | async-done | bytes 1048592 | tf_op jit(solution)/shard_map/reduce_scatter | solution.py:64
  378.8 21.5 %all-gather.12.cloned.1.call-done = bf16[256,2048]{1,0:T(8,128)(2,1)} async-done(((bf16[256,1024]{1,0:T(8,128)(2,1)}), bf16[256,2048]{1,0:T(8,128)(2,1)}) %all-gather.12.cloned.1.call-update) | async-done | bytes 1048592 | tf_op jit(solution)/shard_map/all_gather | solution.py:76
  401.8 7.6 %fusion.111 = f32[256,3584]{1,0:T(8,128)S(1)} fusion(bf16[256,2048]{1,0:T(8,128)(2,1)} %all-gather.12.cloned.1.call-done, bf16[3584,2048]{1,0:T(8,128)(2,1)} %all-gather.8.cloned.1.call-done), kind=kOutput, calls=%fused_computation.153 | convolution fusion | flops 3758096384 | bytes 19398656 | tf_op jit(solution)/shard_map/dot_general | solution.py:20
  414.9 7.0 %psum.80 = bf16[256,16]{0,1:T(8,128)(2,1)S(1)} all-reduce(f32[256,16]{0,1:T(8,128)S(1)} %convolution_multiply_fusion.14), channel_id=1, replica_groups=mesh['client'=16,'tp'=2] {'tp'}, use_global_device_ids=true, to_apply=%region_6.7 | all-reduce | flops 4096 | bytes 24576 | tf_op jit(solution)/shard_map/psum | solution.py:87
  428.9 8.7 %fusion.112 = f32[256,2048]{1,0:T(8,128)} fusion(bf16[256,3584]{1,0:T(8,128)(2,1)S(1)} %get-tuple-element.14, bf16[3584,2048]{1,0:T(8,128)(2,1)} %all-gather.8.cloned.1.call-done), kind=kOutput, calls=%fused_computation.154 | convolution fusion | flops 3758096384 | bytes 18612224 | tf_op jit(solution)/shard_map/dot_general | solution.py:60
  441.9 8.9 %psum.81 = bf16[256,16]{0,1:T(8,128)(2,1)S(1)} all-reduce(f32[256,16]{0,1:T(8,128)S(1)} %fusion.69), channel_id=1, replica_groups=mesh['client'=16,'tp'=2] {'tp'}, use_global_device_ids=true, to_apply=%region_8.9 | all-reduce | flops 4096 | bytes 24576 | tf_op jit(solution)/shard_map/psum | solution.py:65
  452.9 18.1 %reduce-scatter.8.cloned.1.call-done = f32[256,1024]{1,0:T(8,128)} async-done(((f32[256,2048]{1,0:T(8,128)}), f32[256,1024]{1,0:T(8,128)}) %reduce-scatter.8.cloned.1.call-update) | async-done | bytes 1048592 | tf_op jit(solution)/shard_map/reduce_scatter | solution.py:64
  474.3 20.8 %all-gather.14.cloned.1.call-done = bf16[256,2048]{1,0:T(8,128)(2,1)} async-done(((bf16[256,1024]{1,0:T(8,128)(2,1)}), bf16[256,2048]{1,0:T(8,128)(2,1)}) %all-gather.14.cloned.1.call-update) | async-done | bytes 1048592 | tf_op jit(solution)/shard_map/all_gather | solution.py:76
  498.7 7.6 %fusion.113 = f32[256,3584]{1,0:T(8,128)S(1)} fusion(bf16[256,2048]{1,0:T(8,128)(2,1)} %all-gather.14.cloned.1.call-done, bf16[3584,2048]{1,0:T(8,128)(2,1)} %all-gather.8.cloned.1.call-done), kind=kOutput, calls=%fused_computation.155 | convolution fusion | flops 3758096384 | bytes 19398656 | tf_op jit(solution)/shard_map/dot_general | solution.py:20
  506.4 3.7 fusion.11
  511.8 7.0 %psum.82 = bf16[256,16]{0,1:T(8,128)(2,1)S(1)} all-reduce(f32[256,16]{0,1:T(8,128)S(1)} %convolution_multiply_fusion.12), channel_id=1, replica_groups=mesh['client'=16,'tp'=2] {'tp'}, use_global_device_ids=true, to_apply=%region_9.10 | all-reduce | flops 4096 | bytes 24576 | tf_op jit(solution)/shard_map/psum | solution.py:87
  520.9 32.8 %psum.84 = f32[1]{0:T(128)} all-reduce(f32[1]{0:T(128)} %convert_element_type.118), channel_id=1, replica_groups=mesh['client'=16,'tp'=2] {'client'}, use_global_device_ids=true, to_apply=%region_11.12 | all-reduce | flops 1 | bytes 8 | tf_op jit(solution)/shard_map/psum | solution.py:104
  554.4 60.0 %all-reduce.3.cloned.1.call-done = (f32[16,2048]{1,0:T(8,128)}, f32[16,3584]{1,0:T(8,128)}, f32[16,3584]{1,0:T(8,128)}, f32[16,2048]{1,0:T(8,128)}) async-done(((f32[16,2048]{1,0:T(8,128)}, f32[16,3584]{1,0:T(8,128)}, f32[16,3584]{1,0:T(8,128)}, f32[16,2048]{1,0:T(8,128)}), (f32[16,2048]{1,0:T(8,128)}, f32[16,3584]{1,0:T(8,128)}, f32[16,3584]{1,0:T(8,128)}, ...) | async-done | bytes 720912 | tf_op jit(solution)/shard_map/psum | solution.py:104
  (135 shorter events, 66.1 us)
Async XLA Ops:
  7.2 119.2 %copy-start.3 = (bf16[256,2048]{1,0:T(8,128)(2,1)S(1)}, bf16[256,2048]{1,0:T(8,128)(2,1)}, u32[]{:S(2)}) copy-start(bf16[256,2048]{1,0:T(8,128)(2,1)} %param.10) | copy-start | bytes 3145732
  7.2 119.2 %copy-start.30 = (f32[2048]{0:T(1024)S(1)}, f32[2048]{0:T(1024)}, u32[]{:S(2)}) copy-start(f32[2048]{0:T(1024)} %param.12) | copy-start | bytes 24580
  7.2 119.2 %all-gather.6.cloned.1.call-start = ((), (), s32[]{:S(2)}) async-start(), calls=%async_computation.3 | async-start | bytes 15597568 | tf_op jit(solution)/shard_map/all_gather | solution.py:45
  7.9 235.5 %all-gather.8.cloned.1.call-start = ((), (), s32[]{:S(2)}) async-start(), calls=%async_computation.4 | async-start | bytes 15597568 | tf_op jit(solution)/shard_map/all_gather | solution.py:47
  8.7 274.0 %reduce-scatter.4.cloned.1.call-start = ((), (), s32[]{:S(2)}) async-start(), calls=%async_computation.5 | async-start | bytes 3145728 | tf_op jit(solution)/shard_map/reduce_scatter | solution.py:64
  10.2 123.5 %copy-start.24 = (f32[256]{0:T(256)}, f32[256]{0:T(256)S(1)}, u32[]{:S(2)}) copy-start(f32[256]{0:T(256)S(1)} %add_rsqrt_fusion) | copy-start | bytes 3076
  11.9 121.8 %copy-start.18 = (bf16[256,16]{0,1:T(8,128)(2,1)}, bf16[256,16]{0,1:T(8,128)(2,1)S(1)}, u32[]{:S(2)}) copy-start(bf16[256,16]{0,1:T(8,128)(2,1)S(1)} %convolution_convert_fusion.2) | copy-start | bytes 24580
  11.9 123.7 %copy-start.7 = (f32[16,3584]{1,0:T(8,128)S(1)}, f32[16,3584]{1,0:T(8,128)}, u32[]{:S(2)}) copy-start(f32[16,3584]{1,0:T(8,128)} %param.16) | copy-start | bytes 688132
  138.7 113.6 %copy-start = (bf16[256,3584]{1,0:T(8,128)(2,1)}, bf16[256,3584]{1,0:T(8,128)(2,1)S(1)}, u32[]{:S(2)}) copy-start(bf16[256,3584]{1,0:T(8,128)(2,1)S(1)} %get-tuple-element.8) | copy-start | bytes 5505028
  243.4 8.8 %copy-start.8 = (f32[16,2048]{1,0:T(8,128)S(1)}, f32[16,2048]{1,0:T(8,128)}, u32[]{:S(2)}) copy-start(f32[16,2048]{1,0:T(8,128)} %param.18) | copy-start | bytes 393220
  243.4 8.9 %copy-start.6 = (f32[16,3584]{1,0:T(8,128)S(1)}, f32[16,3584]{1,0:T(8,128)}, u32[]{:S(2)}) copy-start(f32[16,3584]{1,0:T(8,128)} %param.17) | copy-start | bytes 688132
  252.2 54.3 %all-gather.10.cloned.1.call-start = ((), (), s32[]{:S(2)}) async-start(), calls=%async_computation.6 | async-start | bytes 1572864 | tf_op jit(solution)/shard_map/all_gather | solution.py:76
  285.2 90.9 %reduce-scatter.6.cloned.1.call-start = ((), (), s32[]{:S(2)}) async-start(), calls=%async_computation.7 | async-start | bytes 3145728 | tf_op jit(solution)/shard_map/reduce_scatter | solution.py:64
  306.5 9.5 %copy-start.4 = (bf16[256,2048]{1,0:T(8,128)(2,1)S(1)}, bf16[256,2048]{1,0:T(8,128)(2,1)}, u32[]{:S(2)}) copy-start(bf16[256,2048]{1,0:T(8,128)(2,1)} %all-gather.10.cloned.1.call-done) | copy-start | bytes 3145732
  342.8 57.5 %all-gather.12.cloned.1.call-start = ((), (), s32[]{:S(2)}) async-start(), calls=%async_computation.8 | async-start | bytes 1572864 | tf_op jit(solution)/shard_map/all_gather | solution.py:76
  378.7 92.3 %reduce-scatter.8.cloned.1.call-start = ((), (), s32[]{:S(2)}) async-start(), calls=%async_computation.9 | async-start | bytes 3145728 | tf_op jit(solution)/shard_map/reduce_scatter | solution.py:64
  437.7 57.4 %all-gather.14.cloned.1.call-start = ((), (), s32[]{:S(2)}) async-start(), calls=%async_computation.10 | async-start | bytes 1572864 | tf_op jit(solution)/shard_map/all_gather | solution.py:76
  439.7 57.0 %copy-start.2 = (bf16[256,3584]{1,0:T(8,128)(2,1)S(1)}, bf16[256,3584]{1,0:T(8,128)(2,1)}, u32[]{:S(2)}) copy-start(bf16[256,3584]{1,0:T(8,128)(2,1)} %copy-done.1) | copy-start | bytes 5505028
  473.6 140.7 %all-reduce.3.cloned.1.call-start = ((), (), s32[]{:S(2)}) async-start(), calls=%async_computation.11 | async-start | bytes 1441792 | tf_op jit(solution)/shard_map/psum | solution.py:104
  510.1 8.7 %copy-start.27 = (f32[256]{0:T(256)S(1)}, f32[256]{0:T(256)}, u32[]{:S(2)}) copy-start(f32[256]{0:T(256)} %copy-done.24) | copy-start | bytes 3076
  510.1 8.7 %copy-start.29 = (f32[16,2048]{1,0:T(8,128)S(1)}, f32[16,2048]{1,0:T(8,128)}, u32[]{:S(2)}) copy-start(f32[16,2048]{1,0:T(8,128)} %param.15) | copy-start | bytes 393220
  510.1 8.7 %copy-start.33 = (f32[2048]{0:T(1024)S(1)}, f32[2048]{0:T(1024)}, u32[]{:S(2)}) copy-start(f32[2048]{0:T(1024)} %param.12) | copy-start | bytes 24580
  510.2 9.8 %copy-start.5 = (bf16[256,2048]{1,0:T(8,128)(2,1)S(1)}, bf16[256,2048]{1,0:T(8,128)(2,1)}, u32[]{:S(2)}) copy-start(bf16[256,2048]{1,0:T(8,128)(2,1)} %all-gather.14.cloned.1.call-done) | copy-start | bytes 3145732
  510.2 9.8 %copy-start.17 = (f32[16,2048]{1,0:T(8,128)S(1)}, f32[16,2048]{1,0:T(8,128)}, u32[]{:S(2)}) copy-start(f32[16,2048]{1,0:T(8,128)} %get-tuple-element.17) | copy-start | bytes 393220
  (25 other events, 107.0 us)
Sparse Core Ops, SparseCore 0:
  10.3 116.0 all-gather.5
  128.5 114.8 all-gather.7
  252.3 30.3 reduce-scatter.3
  285.4 21.0 all-gather.9
  342.9 33.1 reduce-scatter.5
  378.8 21.3 all-gather.11
  437.8 33.1 reduce-scatter.7
  473.7 21.3 all-gather.13
  521.0 93.3 all-reduce.2
where the time goes:
time: 625 us; the launch traced here: 624 us
  waiting for transfers between devices  401 us (64%)
  matrix products  115 us (18%)
  blocking collectives  81 us (13%)
  between operations  15.6 us (2%)
  local copies, waits for them, and re-layouts  6.61 us (1%)
    all_gather x1, waiting for transfers between devices, per_device(): whole_up = lax.all_gather(up_frozen, 'client', axis=0, tiled=True)  114 us
    all_gather x1, waiting for transfers between devices, per_device(): whole_down = lax.all_gather(down_frozen, 'client', axis=1, tiled=True)  105 us
    all_gather x3, waiting for transfers between devices, per_device(): output_gradient = lax.all_gather(d_share, 'tp', axis=1, tiled=True)  63.5 us
    psum x1, waiting for transfers between devices, per_device(): lax.psum((deltas[0], deltas[1], deltas[2], deltas[3], weight), 'client')  60 us
    reduce_scatter x3, waiting for transfers between devices, per_device(): lax.psum_scatter(partial_value, 'tp', scatter_dimension=1, tiled=True)  57.1 us
    dot_general x15, matrix products, contract_columns(): lax.dot_general(left, right, (((1,), (1,)), ((), ())), preferred_element_...  36.5 us
    psum x1, blocking collectives, per_device(): lax.psum((deltas[0], deltas[1], deltas[2], deltas[3], weight), 'client')  32.8 us
    psum x3, blocking collectives, per_device(): down_low_product = lax.psum(low_part, 'tp').astype(jnp.bfloat16)  27.1 us
  transfers between devices with their start and end apart: 9, of which 9 were waited for; matrix products, arithmetic and copies ran while one was open for 4% of the time, Pallas kernels for 0%

commit v1 on v0

--- a/solution.py
+++ b/solution.py
@@ -8,6 +8,16 @@
 PROX_WEIGHT = 10.0
 ADAPTER_SCALING = 0.5
 NORM_EPS = 1e-05
+
+
+def gather_by_hops(x, mesh_axis, dim):
+    peers = lax.axis_size(mesh_axis)
+    held, blocks = (x, [x])
+    for _ in range(peers - 1):
+        held = lax.ppermute(held, mesh_axis, [(i, (i + 1) % peers) for i in range(peers)])
+        blocks.insert(0, held)
+    flat = jnp.concatenate(blocks, axis=dim)
+    return jnp.roll(flat, (lax.axis_index(mesh_axis) + 1) * x.shape[dim], axis=dim)
 
 
 def contracted_rows(left, right):
@@ -44,7 +54,7 @@
     normalized_input = (wide * scale * norm_gain).astype(jnp.bfloat16)
     whole_up = lax.all_gather(up_frozen, "client", axis=0, tiled=True)
     frozen_hidden_rows = jnp.dot(normalized_input, whole_up, preferred_element_type=jnp.float32)
-    whole_down = lax.all_gather(down_frozen, "client", axis=1, tiled=True)
+    whole_down = gather_by_hops(down_frozen, "client", 1)
     start = (up_left, up_right, down_left, down_right)
     params = start
     for local_step in range(STEPS):

time: 625 us -> 774 us (1.24); the launches traced: 624 us -> 765 us
  waiting for transfers between devices: 401 us -> 473 us
  local copies, waits for them, and re-layouts: 6.61 us -> 51.6 us
  matrix products: 115 us -> 127 us
  other arithmetic: 5.07 us -> 12.9 us
    ppermute x0 -> x15, waiting for transfers between devices: none -> 294 us  [gather_by_hops(): lax.ppermute(held, mesh_axis, [(i, (i + 1) % peers) for i in range(peers)])]
    all_gather x1, waiting for transfers between devices: 114 us -> 0.01 us  [per_device(): whole_up = lax.all_gather(up_frozen, 'client', axis=0, tiled=True)]
    all_gather x1 -> x0, waiting for transfers between devices: 105 us -> none  [per_device(): whole_down = lax.all_gather(down_frozen, 'client', axis=1, tiled=True)]
    unnamed x80 -> x145, local copies, waits for them, and re-layouts: 6.61 us -> 50.6 us
    dot_general x15, matrix products: 36.5 us -> 51.9 us  [contract_columns(): lax.dot_general(left, right, (((1,), (1,)), ((), ())), preferred_element_...]
    convert_element_type x0 -> x3, other arithmetic: none -> 7.76 us  [per_device(): ((layer_output - target_share.astype(jnp.float32)) / token_count).astype(...]
  transfers between devices with their start and end apart: 9 -> 23, of which waited for: 9 -> 22; matrix products, arithmetic and copies ran while one was open for 4% -> 7% of each run, Pallas kernels for 0% -> 0%
where the time goes in v1:
time: 774 us; the launch traced here: 765 us
  waiting for transfers between devices  473 us (61%)
  matrix products  127 us (16%)
  blocking collectives  83.4 us (11%)
  local copies, waits for them, and re-layouts  51.6 us (7%)
  between operations  16.1 us (2%)
  other arithmetic  12.9 us (2%)
    ppermute x15, waiting for transfers between devices, gather_by_hops(): lax.ppermute(held, mesh_axis, [(i, (i + 1) % peers) for i in range(peers)])  294 us
    all_gather x3, waiting for transfers between devices, per_device(): output_gradient = lax.all_gather(d_share, 'tp', axis=1, tiled=True)  62.6 us
    psum x1, waiting for transfers between devices, per_device(): lax.psum((deltas[0], deltas[1], deltas[2], deltas[3], weight), 'client')  60 us
    reduce_scatter x3, waiting for transfers between devices, per_device(): lax.psum_scatter(partial_value, 'tp', scatter_dimension=1, tiled=True)  55.5 us
    dot_general x15, matrix products, contract_columns(): lax.dot_general(left, right, (((1,), (1,)), ((), ())), preferred_element_...  51.9 us
    unnamed x145, local copies, waits for them, and re-layouts  50.6 us
    psum x1, blocking collectives, per_device(): lax.psum((deltas[0], deltas[1], deltas[2], deltas[3], weight), 'client')  32.9 us
    psum x3, blocking collectives, per_device(): down_low_product = lax.psum(low_part, 'tp').astype(jnp.bfloat16)  29.4 us
  transfers between devices with their start and end apart: 23, of which 22 were waited for; matrix products, arithmetic and copies ran while one was open for 7% of the time, Pallas kernels for 0%

profile of v1, /device:TPU:0, one launch (start us, length us, event | category | flops | bytes accessed | tf_op | source)
XLA Modules:
  0.0 765.4 jit_solution(12327661754922091802)
XLA Ops:
  7.8 16.3 %collective-permute-done = bf16[3584,128]{1,0:T(8,128)(2,1)S(1)} collective-permute-done((bf16[3584,128]{1,0:T(8,128)(2,1)}, bf16[3584,128]{1,0:T(8,128)(2,1)S(1)}, u32[]{:S(2)}, u32[]{:S(2)}) %collective-permute-start) | collective-permute-done | bytes 917536 | tf_op jit(solution)/shard_map/ppermute | solution.py:17
  24.1 15.6 %collective-permute-done.1 = bf16[3584,128]{1,0:T(8,128)(2,1)S(1)} collective-permute-done((bf16[3584,128]{1,0:T(8,128)(2,1)S(1)}, bf16[3584,128]{1,0:T(8,128)(2,1)S(1)}, u32[]{:S(2)}, u32[]{:S(2)}) %collective-permute-start.1) | collective-permute-done | bytes 917536 | tf_op jit(solution)/shard_map/ppermute | solution.py:17
  39.7 35.3 %collective-permute-done.2 = bf16[3584,128]{1,0:T(8,128)(2,1)S(1)} collective-permute-done((bf16[3584,128]{1,0:T(8,128)(2,1)S(1)}, bf16[3584,128]{1,0:T(8,128)(2,1)S(1)}, u32[]{:S(2)}, u32[]{:S(2)}) %collective-permute-start.2) | collective-permute-done | bytes 917536 | tf_op jit(solution)/shard_map/ppermute | solution.py:17
  75.0 22.2 %collective-permute-done.3 = bf16[3584,128]{1,0:T(8,128)(2,1)S(1)} collective-permute-done((bf16[3584,128]{1,0:T(8,128)(2,1)S(1)}, bf16[3584,128]{1,0:T(8,128)(2,1)S(1)}, u32[]{:S(2)}, u32[]{:S(2)}) %collective-permute-start.3) | collective-permute-done | bytes 917536 | tf_op jit(solution)/shard_map/ppermute | solution.py:17
  98.1 35.3 %collective-permute-done.4 = bf16[3584,128]{1,0:T(8,128)(2,1)S(1)} collective-permute-done((bf16[3584,128]{1,0:T(8,128)(2,1)S(1)}, bf16[3584,128]{1,0:T(8,128)(2,1)S(1)}, u32[]{:S(2)}, u32[]{:S(2)}) %collective-permute-start.4) | collective-permute-done | bytes 917536 | tf_op jit(solution)/shard_map/ppermute | solution.py:17
  134.4 33.1 %collective-permute-done.5 = bf16[3584,128]{1,0:T(8,128)(2,1)S(1)} collective-permute-done((bf16[3584,128]{1,0:T(8,128)(2,1)S(1)}, bf16[3584,128]{1,0:T(8,128)(2,1)S(1)}, u32[]{:S(2)}, u32[]{:S(2)}) %collective-permute-start.5) | collective-permute-done | bytes 917536 | tf_op jit(solution)/shard_map/ppermute | solution.py:17
  168.4 15.5 %collective-permute-done.6 = bf16[3584,128]{1,0:T(8,128)(2,1)S(1)} collective-permute-done((bf16[3584,128]{1,0:T(8,128)(2,1)S(1)}, bf16[3584,128]{1,0:T(8,128)(2,1)S(1)}, u32[]{:S(2)}, u32[]{:S(2)}) %collective-permute-start.6) | collective-permute-done | bytes 917536 | tf_op jit(solution)/shard_map/ppermute | solution.py:17
  184.8 15.5 %collective-permute-done.7 = bf16[3584,128]{1,0:T(8,128)(2,1)S(1)} collective-permute-done((bf16[3584,128]{1,0:T(8,128)(2,1)S(1)}, bf16[3584,128]{1,0:T(8,128)(2,1)S(1)}, u32[]{:S(2)}, u32[]{:S(2)}) %collective-permute-start.7) | collective-permute-done | bytes 917536 | tf_op jit(solution)/shard_map/ppermute | solution.py:17
  201.3 15.5 %collective-permute-done.8 = bf16[3584,128]{1,0:T(8,128)(2,1)S(1)} collective-permute-done((bf16[3584,128]{1,0:T(8,128)(2,1)S(1)}, bf16[3584,128]{1,0:T(8,128)(2,1)S(1)}, u32[]{:S(2)}, u32[]{:S(2)}) %collective-permute-start.8) | collective-permute-done | bytes 917536 | tf_op jit(solution)/shard_map/ppermute | solution.py:17
  217.8 15.5 %collective-permute-done.9 = bf16[3584,128]{1,0:T(8,128)(2,1)S(1)} collective-permute-done((bf16[3584,128]{1,0:T(8,128)(2,1)S(1)}, bf16[3584,128]{1,0:T(8,128)(2,1)S(1)}, u32[]{:S(2)}, u32[]{:S(2)}) %collective-permute-start.9) | collective-permute-done | bytes 917536 | tf_op jit(solution)/shard_map/ppermute | solution.py:17
  234.2 15.5 %collective-permute-done.10 = bf16[3584,128]{1,0:T(8,128)(2,1)S(1)} collective-permute-done((bf16[3584,128]{1,0:T(8,128)(2,1)S(1)}, bf16[3584,128]{1,0:T(8,128)(2,1)S(1)}, u32[]{:S(2)}, u32[]{:S(2)}) %collective-permute-start.10) | collective-permute-done | bytes 917536 | tf_op jit(solution)/shard_map/ppermute | solution.py:17
  250.7 15.5 %collective-permute-done.11 = bf16[3584,128]{1,0:T(8,128)(2,1)S(1)} collective-permute-done((bf16[3584,128]{1,0:T(8,128)(2,1)S(1)}, bf16[3584,128]{1,0:T(8,128)(2,1)S(1)}, u32[]{:S(2)}, u32[]{:S(2)}) %collective-permute-start.11) | collective-permute-done | bytes 917536 | tf_op jit(solution)/shard_map/ppermute | solution.py:17
  267.1 15.5 %collective-permute-done.12 = bf16[3584,128]{1,0:T(8,128)(2,1)S(1)} collective-permute-done((bf16[3584,128]{1,0:T(8,128)(2,1)S(1)}, bf16[3584,128]{1,0:T(8,128)(2,1)S(1)}, u32[]{:S(2)}, u32[]{:S(2)}) %collective-permute-start.12) | collective-permute-done | bytes 917536 | tf_op jit(solution)/shard_map/ppermute | solution.py:17
  283.6 15.6 %collective-permute-done.13 = bf16[3584,128]{1,0:T(8,128)(2,1)} collective-permute-done((bf16[3584,128]{1,0:T(8,128)(2,1)S(1)}, bf16[3584,128]{1,0:T(8,128)(2,1)}, u32[]{:S(2)}, u32[]{:S(2)}) %collective-permute-start.13) | collective-permute-done | bytes 917536 | tf_op jit(solution)/shard_map/ppermute | solution.py:17
  302.6 12.4 %collective-permute-done.14 = bf16[3584,128]{1,0:T(8,128)(2,1)} collective-permute-done((bf16[3584,128]{1,0:T(8,128)(2,1)}, bf16[3584,128]{1,0:T(8,128)(2,1)}, u32[]{:S(2)}, u32[]{:S(2)}) %collective-permute-start.14) | collective-permute-done | bytes 917536 | tf_op jit(solution)/shard_map/ppermute | solution.py:17
  386.2 19.7 %reduce-scatter.4.cloned.1.call-done = f32[256,1024]{1,0:T(8,128)} async-done(((f32[256,2048]{1,0:T(8,128)}), f32[256,1024]{1,0:T(8,128)}) %reduce-scatter.4.cloned.1.call-update) | async-done | bytes 1048592 | tf_op jit(solution)/shard_map/reduce_scatter | solution.py:74
  408.9 20.9 %all-gather.7.cloned.1.call-done = bf16[256,2048]{1,0:T(8,128)(2,1)} async-done(((bf16[256,1024]{1,0:T(8,128)(2,1)}), bf16[256,2048]{1,0:T(8,128)(2,1)}) %all-gather.7.cloned.1.call-update) | async-done | bytes 1048592 | tf_op jit(solution)/shard_map/all_gather | solution.py:86
  484.7 17.9 %reduce-scatter.6.cloned.1.call-done = f32[256,1024]{1,0:T(8,128)} async-done(((f32[256,2048]{1,0:T(8,128)}), f32[256,1024]{1,0:T(8,128)}) %reduce-scatter.6.cloned.1.call-update) | async-done | bytes 1048592 | tf_op jit(solution)/shard_map/reduce_scatter | solution.py:74
  505.7 21.3 %all-gather.9.cloned.1.call-done = bf16[256,2048]{1,0:T(8,128)(2,1)} async-done(((bf16[256,1024]{1,0:T(8,128)(2,1)}), bf16[256,2048]{1,0:T(8,128)(2,1)}) %all-gather.9.cloned.1.call-update) | async-done | bytes 1048592 | tf_op jit(solution)/shard_map/all_gather | solution.py:86
  532.0 13.5 %fusion.45 = bf16[256,3584]{1,0:T(8,128)(2,1)} fusion(f32[256,3584]{1,0:T(8,128)} %fusion.113, bf16[256,2048]{1,0:T(8,128)(2,1)} %all-gather.9.cloned.1.call-done, bf16[3584,4096]{1,0:T(8,128)(2,1)} %constant_dynamic-update-slice_fusion, s32[]{:T(128)S(6)} %select_n.26, f32[256,3584]{1,0:T(8,128)} %get-tuple-element.13), kind=kOutput, calls=%fused_computation.28 | convolution fusion | flops 3767271424 | bytes 24903684 | tf_op jit(solution)/shard_map/dot_general | solution.py:30
  587.9 17.9 %reduce-scatter.8.cloned.1.call-done = f32[256,1024]{1,0:T(8,128)} async-done(((f32[256,2048]{1,0:T(8,128)}), f32[256,1024]{1,0:T(8,128)}) %reduce-scatter.8.cloned.1.call-update) | async-done | bytes 1048592 | tf_op jit(solution)/shard_map/reduce_scatter | solution.py:74
  609.3 20.5 %all-gather.11.cloned.1.call-done = bf16[256,2048]{1,0:T(8,128)(2,1)} async-done(((bf16[256,1024]{1,0:T(8,128)(2,1)}), bf16[256,2048]{1,0:T(8,128)(2,1)}) %all-gather.11.cloned.1.call-update) | async-done | bytes 1048592 | tf_op jit(solution)/shard_map/all_gather | solution.py:86
  661.2 32.9 %psum.84 = f32[1]{0:T(128)} all-reduce(f32[1]{0:T(128)} %convert_element_type.118), channel_id=1, replica_groups=mesh['client'=16,'tp'=2] {'client'}, use_global_device_ids=true, to_apply=%region_11.12 | all-reduce | flops 1 | bytes 8 | tf_op jit(solution)/shard_map/psum | solution.py:114
  694.8 60.0 %all-reduce.3.cloned.1.call-done = (f32[16,2048]{1,0:T(8,128)}, f32[16,3584]{1,0:T(8,128)}, f32[16,3584]{1,0:T(8,128)}, f32[16,2048]{1,0:T(8,128)}) async-done(((f32[16,2048]{1,0:T(8,128)}, f32[16,3584]{1,0:T(8,128)}, f32[16,3584]{1,0:T(8,128)}, f32[16,2048]{1,0:T(8,128)}), (f32[16,2048]{1,0:T(8,128)}, f32[16,3584]{1,0:T(8,128)}, f32[16,3584]{1,0:T(8,128)}, ...) | async-done | bytes 720912 | tf_op jit(solution)/shard_map/psum | solution.py:114
  (231 shorter events, 230.4 us)
Async XLA Ops:
  7.2 346.4 %all-gather.5.cloned.1.call-start = ((), (), s32[]{:S(2)}) async-start(), calls=%async_computation.3 | async-start | bytes 15597568 | tf_op jit(solution)/shard_map/all_gather | solution.py:55
  7.2 16.8 %collective-permute-start = (bf16[3584,128]{1,0:T(8,128)(2,1)}, bf16[3584,128]{1,0:T(8,128)(2,1)S(1)}, u32[]{:S(2)}, u32[]{:S(2)}) collective-permute-start(bf16[3584,128]{1,0:T(8,128)(2,1)} %param.14), channel_id=1, source_target_pairs={{0,2},{2,4},{4,6},{6,8},{8,10},{10,12},{12,14},{14,16},{16,18},{18... | collective-permute-start | bytes 2752520 | tf_op jit(solution)/shard_map/ppermute | solution.py:17
  24.0 15.6 %collective-permute-start.1 = (bf16[3584,128]{1,0:T(8,128)(2,1)S(1)}, bf16[3584,128]{1,0:T(8,128)(2,1)S(1)}, u32[]{:S(2)}, u32[]{:S(2)}) collective-permute-start(bf16[3584,128]{1,0:T(8,128)(2,1)S(1)} %collective-permute-done), channel_id=1, source_target_pairs={{0,2},{2,4},{4,6},{6,8},{8,10},{10,12},{12,14},{14,16},{16,18},{18... | collective-permute-start | bytes 2752520 | tf_op jit(solution)/shard_map/ppermute | solution.py:17
  24.1 381.9 %reduce-scatter.4.cloned.1.call-start = ((), (), s32[]{:S(2)}) async-start(), calls=%async_computation.4 | async-start | bytes 3145728 | tf_op jit(solution)/shard_map/reduce_scatter | solution.py:74
  39.7 35.3 %collective-permute-start.2 = (bf16[3584,128]{1,0:T(8,128)(2,1)S(1)}, bf16[3584,128]{1,0:T(8,128)(2,1)S(1)}, u32[]{:S(2)}, u32[]{:S(2)}) collective-permute-start(bf16[3584,128]{1,0:T(8,128)(2,1)S(1)} %collective-permute-done.1), channel_id=1, source_target_pairs={{0,2},{2,4},{4,6},{6,8},{8,10},{10,12},{12,14},{14,16},{16,18},{18... | collective-permute-start | bytes 2752520 | tf_op jit(solution)/shard_map/ppermute | solution.py:17
  75.0 255.3 %copy-start.7 = (bf16[3584,128]{1,0:T(8,128)(2,1)}, bf16[3584,128]{1,0:T(8,128)(2,1)S(1)}, u32[]{:S(2)}) copy-start(bf16[3584,128]{1,0:T(8,128)(2,1)S(1)} %collective-permute-done.2) | copy-start | bytes 2752516
  75.0 22.2 %collective-permute-start.3 = (bf16[3584,128]{1,0:T(8,128)(2,1)S(1)}, bf16[3584,128]{1,0:T(8,128)(2,1)S(1)}, u32[]{:S(2)}, u32[]{:S(2)}) collective-permute-start(bf16[3584,128]{1,0:T(8,128)(2,1)S(1)} %collective-permute-done.2), channel_id=1, source_target_pairs={{0,2},{2,4},{4,6},{6,8},{8,10},{10,12},{12,14},{14,16},{16,18},{18... | collective-permute-start | bytes 2752520 | tf_op jit(solution)/shard_map/ppermute | solution.py:17
  98.1 35.3 %collective-permute-start.4 = (bf16[3584,128]{1,0:T(8,128)(2,1)S(1)}, bf16[3584,128]{1,0:T(8,128)(2,1)S(1)}, u32[]{:S(2)}, u32[]{:S(2)}) collective-permute-start(bf16[3584,128]{1,0:T(8,128)(2,1)S(1)} %collective-permute-done.3), channel_id=1, source_target_pairs={{0,2},{2,4},{4,6},{6,8},{8,10},{10,12},{12,14},{14,16},{16,18},{18... | collective-permute-start | bytes 2752520 | tf_op jit(solution)/shard_map/ppermute | solution.py:17
  134.4 33.1 %collective-permute-start.5 = (bf16[3584,128]{1,0:T(8,128)(2,1)S(1)}, bf16[3584,128]{1,0:T(8,128)(2,1)S(1)}, u32[]{:S(2)}, u32[]{:S(2)}) collective-permute-start(bf16[3584,128]{1,0:T(8,128)(2,1)S(1)} %collective-permute-done.4), channel_id=1, source_target_pairs={{0,2},{2,4},{4,6},{6,8},{8,10},{10,12},{12,14},{14,16},{16,18},{18... | collective-permute-start | bytes 2752520 | tf_op jit(solution)/shard_map/ppermute | solution.py:17
  168.4 15.5 %collective-permute-start.6 = (bf16[3584,128]{1,0:T(8,128)(2,1)S(1)}, bf16[3584,128]{1,0:T(8,128)(2,1)S(1)}, u32[]{:S(2)}, u32[]{:S(2)}) collective-permute-start(bf16[3584,128]{1,0:T(8,128)(2,1)S(1)} %collective-permute-done.5), channel_id=1, source_target_pairs={{0,2},{2,4},{4,6},{6,8},{8,10},{10,12},{12,14},{14,16},{16,18},{18... | collective-permute-start | bytes 2752520 | tf_op jit(solution)/shard_map/ppermute | solution.py:17
  184.8 15.5 %collective-permute-start.7 = (bf16[3584,128]{1,0:T(8,128)(2,1)S(1)}, bf16[3584,128]{1,0:T(8,128)(2,1)S(1)}, u32[]{:S(2)}, u32[]{:S(2)}) collective-permute-start(bf16[3584,128]{1,0:T(8,128)(2,1)S(1)} %collective-permute-done.6), channel_id=1, source_target_pairs={{0,2},{2,4},{4,6},{6,8},{8,10},{10,12},{12,14},{14,16},{16,18},{18... | collective-permute-start | bytes 2752520 | tf_op jit(solution)/shard_map/ppermute | solution.py:17
  201.3 15.5 %collective-permute-start.8 = (bf16[3584,128]{1,0:T(8,128)(2,1)S(1)}, bf16[3584,128]{1,0:T(8,128)(2,1)S(1)}, u32[]{:S(2)}, u32[]{:S(2)}) collective-permute-start(bf16[3584,128]{1,0:T(8,128)(2,1)S(1)} %collective-permute-done.7), channel_id=1, source_target_pairs={{0,2},{2,4},{4,6},{6,8},{8,10},{10,12},{12,14},{14,16},{16,18},{18... | collective-permute-start | bytes 2752520 | tf_op jit(solution)/shard_map/ppermute | solution.py:17
  217.7 15.5 %collective-permute-start.9 = (bf16[3584,128]{1,0:T(8,128)(2,1)S(1)}, bf16[3584,128]{1,0:T(8,128)(2,1)S(1)}, u32[]{:S(2)}, u32[]{:S(2)}) collective-permute-start(bf16[3584,128]{1,0:T(8,128)(2,1)S(1)} %collective-permute-done.8), channel_id=1, source_target_pairs={{0,2},{2,4},{4,6},{6,8},{8,10},{10,12},{12,14},{14,16},{16,18},{18... | collective-permute-start | bytes 2752520 | tf_op jit(solution)/shard_map/ppermute | solution.py:17
  234.2 15.5 %collective-permute-start.10 = (bf16[3584,128]{1,0:T(8,128)(2,1)S(1)}, bf16[3584,128]{1,0:T(8,128)(2,1)S(1)}, u32[]{:S(2)}, u32[]{:S(2)}) collective-permute-start(bf16[3584,128]{1,0:T(8,128)(2,1)S(1)} %collective-permute-done.9), channel_id=1, source_target_pairs={{0,2},{2,4},{4,6},{6,8},{8,10},{10,12},{12,14},{14,16},{16,18},{18... | collective-permute-start | bytes 2752520 | tf_op jit(solution)/shard_map/ppermute | solution.py:17
  250.7 15.5 %collective-permute-start.11 = (bf16[3584,128]{1,0:T(8,128)(2,1)S(1)}, bf16[3584,128]{1,0:T(8,128)(2,1)S(1)}, u32[]{:S(2)}, u32[]{:S(2)}) collective-permute-start(bf16[3584,128]{1,0:T(8,128)(2,1)S(1)} %collective-permute-done.10), channel_id=1, source_target_pairs={{0,2},{2,4},{4,6},{6,8},{8,10},{10,12},{12,14},{14,16},{16,18},{18... | collective-permute-start | bytes 2752520 | tf_op jit(solution)/shard_map/ppermute | solution.py:17
  267.1 15.5 %collective-permute-start.12 = (bf16[3584,128]{1,0:T(8,128)(2,1)S(1)}, bf16[3584,128]{1,0:T(8,128)(2,1)S(1)}, u32[]{:S(2)}, u32[]{:S(2)}) collective-permute-start(bf16[3584,128]{1,0:T(8,128)(2,1)S(1)} %collective-permute-done.11), channel_id=1, source_target_pairs={{0,2},{2,4},{4,6},{6,8},{8,10},{10,12},{12,14},{14,16},{16,18},{18... | collective-permute-start | bytes 2752520 | tf_op jit(solution)/shard_map/ppermute | solution.py:17
  283.6 15.6 %collective-permute-start.13 = (bf16[3584,128]{1,0:T(8,128)(2,1)S(1)}, bf16[3584,128]{1,0:T(8,128)(2,1)}, u32[]{:S(2)}, u32[]{:S(2)}) collective-permute-start(bf16[3584,128]{1,0:T(8,128)(2,1)S(1)} %collective-permute-done.12), channel_id=1, source_target_pairs={{0,2},{2,4},{4,6},{6,8},{8,10},{10,12},{12,14},{14,16},{16,18},{18... | collective-permute-start | bytes 2752520 | tf_op jit(solution)/shard_map/ppermute | solution.py:17
  299.2 15.8 %collective-permute-start.14 = (bf16[3584,128]{1,0:T(8,128)(2,1)}, bf16[3584,128]{1,0:T(8,128)(2,1)}, u32[]{:S(2)}, u32[]{:S(2)}) collective-permute-start(bf16[3584,128]{1,0:T(8,128)(2,1)} %collective-permute-done.13), channel_id=1, source_target_pairs={{0,2},{2,4},{4,6},{6,8},{8,10},{10,12},{12,14},{14,16},{16,18},{18... | collective-permute-start | bytes 2752520 | tf_op jit(solution)/shard_map/ppermute | solution.py:17
  373.6 56.2 %all-gather.7.cloned.1.call-start = ((), (), s32[]{:S(2)}) async-start(), calls=%async_computation.5 | async-start | bytes 1572864 | tf_op jit(solution)/shard_map/all_gather | solution.py:86
  408.4 94.2 %reduce-scatter.6.cloned.1.call-start = ((), (), s32[]{:S(2)}) async-start(), calls=%async_computation.6 | async-start | bytes 3145728 | tf_op jit(solution)/shard_map/reduce_scatter | solution.py:74
  469.3 57.7 %all-gather.9.cloned.1.call-start = ((), (), s32[]{:S(2)}) async-start(), calls=%async_computation.7 | async-start | bytes 1572864 | tf_op jit(solution)/shard_map/all_gather | solution.py:86
  505.5 100.3 %reduce-scatter.8.cloned.1.call-start = ((), (), s32[]{:S(2)}) async-start(), calls=%async_computation.8 | async-start | bytes 3145728 | tf_op jit(solution)/shard_map/reduce_scatter | solution.py:74
  572.4 57.4 %all-gather.11.cloned.1.call-start = ((), (), s32[]{:S(2)}) async-start(), calls=%async_computation.9 | async-start | bytes 1572864 | tf_op jit(solution)/shard_map/all_gather | solution.py:86
  608.3 146.5 %all-reduce.3.cloned.1.call-start = ((), (), s32[]{:S(2)}) async-start(), calls=%async_computation.10 | async-start | bytes 1441792 | tf_op jit(solution)/shard_map/psum | solution.py:114
  (56 other events, 487.7 us)
Sparse Core Ops, SparseCore 0:
  24.2 137.5 all-gather.4
  373.7 32.1 reduce-scatter.3
  408.5 21.1 all-gather.6
  469.4 33.1 reduce-scatter.5
  505.6 21.3 all-gather.8
  572.5 33.1 reduce-scatter.7
  608.4 21.3 all-gather.10
  661.4 93.4 all-reduce.2
